TPU v7x, 32 devices: a whole 2x2x4 slice. The times are simulated.
32 devices in a mesh: half: 2 (over core), blk: 4 (over z), sub: 4 (over y, x).
Axes of the slice: x: 2, y: 2, z: 4, core: 2. Of those that a mesh axis runs over, the one named last changes fastest.
Arguments:
- leaf_expansions: float32 [16384, 128], P(('half', 'blk', 'sub')), may hold values from -0.3 to 0.3
- leaf_occupied: int32 [16384], P(('half', 'blk', 'sub')), may hold values 0 or 1
- cone_angles: float32 [2, 48], replicated, may hold values from -3.140625 to 3.140625
- cone_need3: int32 [48, 32], P(('half', 'blk'), 'sub'), may hold values 0 or 1
- cone_need4: int32 [48, 4], P(('half', 'blk'), 'sub'), may hold values 0 or 1
Outputs:
- lowfreq: float32 [256, 128], P(('half', 'blk', 'sub'))
- cone_expansions: float32 [48, 4, 128], P(('half', 'blk'), 'sub')
All inputs are finite; a program needn't handle non-finite values. No bound on the sum of `leaf_occupied` or of `cone_need3` or of `cone_need4` on one device may be relied on, other than what follows from the above.
Results may differ from a plain program's by a relative error of at most 0.00007.
Values sent between devices are 32-bit elements; how exact they have to be, the bound alone decides.
A program may use at most 64 MiB of HBM per device.

v0:
```python
import functools
import math

import jax
import jax.numpy as jnp
import numpy as np
from jax import lax
from jax.experimental import pallas as pl
from jax.experimental.pallas import tpu as pltpu
from jax.sharding import PartitionSpec as P

MESH = pl.DeviceIdType.MESH
F32, BF16 = jnp.float32, jnp.bfloat16
ORDER = 4
OCT = 8
NEAR = 1.5


def octant_signs():
    octant = np.arange(OCT)
    return np.stack([octant // 4 % 2, octant // 2 % 2, octant % 2], -1) * 2.0 - 1.0


def chebyshev_points(per_axis):
    return np.cos((2.0 * np.arange(per_axis) + 1.0) * math.pi / (2.0 * per_axis))


def octant_table(per_axis):
    points = chebyshev_points(per_axis)
    degree = np.arange(1, per_axis)
    shifted = (points[None, :] + np.array([-1.0, 1.0])[:, None]) / 2.0
    here = np.cos(degree[None, :] * np.arccos(points)[:, None])
    there = np.cos(degree * np.arccos(shifted)[:, :, None])
    single = 1.0 / per_axis + 2.0 / per_axis * np.einsum("mk,bnk->bnm", here, there)
    bit = (octant_signs() > 0).astype(int)
    full = np.einsum("oda,oeb,ofc->odefabc", single[bit[:, 0]], single[bit[:, 1]], single[bit[:, 2]])
    return full.reshape(OCT, per_axis**3, per_axis**3)


def weight_table(per_axis):
    table = octant_table(per_axis).astype(np.float32)
    nodes = per_axis**3
    wide = np.zeros((OCT, 2, nodes, 2, nodes), np.float32)
    wide[:, 0, :, 0, :] = table
    wide[:, 1, :, 1, :] = table
    wide = wide.reshape(OCT * 2 * nodes, 2 * nodes)
    high = wide.astype(BF16)
    low = (wide - high.astype(np.float32)).astype(BF16)
    return np.concatenate([high, low], 1)


def lane_table(per_axis):
    points = chebyshev_points(per_axis)
    index = np.arange(per_axis**3)
    coords = np.stack([points[index // per_axis**2], points[index // per_axis % per_axis], points[index % per_axis]])
    offsets = coords[:, None, :] + octant_signs().T[:, :, None]
    offsets = -NEAR * np.concatenate([offsets, offsets], -1).reshape(3, -1)
    sign = np.tile(np.repeat([-1.0, 1.0], per_axis**3), OCT)
    return np.concatenate([offsets, sign[None]], 0).astype(np.float32)


def each(count, body):
    if count <= 64:
        for d in range(1, count):
            body(d)
    else:
        lax.fori_loop(1, count, lambda d, c: (body(d), c)[1], 0)


def split_rows(value):
    high = value.astype(BF16)
    low = (value - high.astype(F32)).astype(BF16)
    return jnp.concatenate([high, low], 0)


def fold(acc, rows, width):
    return (acc[:rows, :width] + acc[rows:, :width]) + (acc[:rows, width:] + acc[rows:, width:])


def kernel(
    halves, blks, subs, cones,
    leaf_hbm, occ_hbm, angle_hbm, need3_hbm, need4_hbm, weight_hbm, lane_hbm,
    low_out, cone_out,
    leaf, occ, angle, need3, need4, weight, lane, part, got, low, three, phase,
    in_sem, send, recv, send2, recv2,
):
    groups = halves * blks
    half, blk, sub = lax.axis_index("half"), lax.axis_index("blk"), lax.axis_index("sub")
    group = half * blks + blk
    rows, width = leaf.shape
    pairs = rows // (2 * OCT)
    per_sub = pairs // subs

    loads = [
        pltpu.make_async_copy(src, dst, in_sem.at[i])
        for i, (src, dst) in enumerate([
            (occ_hbm, occ), (leaf_hbm, leaf), (weight_hbm, weight), (angle_hbm, angle),
            (lane_hbm, lane), (need3_hbm, need3), (need4_hbm, need4),
        ])
    ]
    for load in loads:
        load.start()

    def peer(d):
        there = lax.rem(blk + d // subs, blks)
        return {"blk": there, "sub": lax.rem(sub + lax.rem(d, subs), subs)}

    def half_peer(e):
        return {"half": lax.rem(half + e, halves)}

    barrier = pltpu.get_barrier_semaphore()

    def greet(target):
        pl.semaphore_signal(barrier, inc=1, device_id=target, device_id_type=MESH)

    each(halves, lambda e: greet(half_peer(e)))
    each(blks * subs, lambda d: greet(peer(d)))

    loads[0].wait()
    loads[1].wait()
    columns = jnp.transpose(occ[...].astype(F32))
    for i in range(rows // 128):
        chunk = pl.ds(i * 128, 128)
        leaf[chunk, :] = leaf[chunk, :] * columns[:, i : i + 1]
    loads[2].wait()
    acc = None
    for t in range(OCT // 2):
        tile = jnp.concatenate(
            [
                jnp.concatenate(
                    [leaf[pl.ds(OCT * r + o, pairs, stride=2 * OCT), :] for o in (2 * t, 2 * t + 1)], 1
                )
                for r in range(2)
            ],
            0,
        )
        term = jnp.dot(
            split_rows(tile), weight[2 * width * t : 2 * width * (t + 1), :], preferred_element_type=F32
        )
        acc = term if acc is None else acc + term
    one = fold(acc, 2 * pairs, width)
    tile = jnp.concatenate([one[:pairs], one[pairs:]], 1)
    mine = weight[pl.ds(pl.multiple_of(sub * 2 * width, 2 * width), 2 * width), :]
    part[...] = fold(jnp.dot(split_rows(tile), mine, preferred_element_type=F32), pairs, width)

    pl.semaphore_wait(barrier, blks * subs + halves - 2)

    def rows_of(index):
        return pl.ds(pl.multiple_of(index * per_sub, 8), per_sub)

    def copy(d):
        return pltpu.make_async_remote_copy(
            src_ref=part.at[rows_of(lax.rem(sub + lax.rem(d, subs), subs))],
            dst_ref=got.at[blk, sub],
            send_sem=send.at[d],
            recv_sem=recv.at[d],
            device_id=peer(d),
            device_id_type=MESH,
        )

    each(blks * subs, lambda d: copy(d).start())
    got[blk, sub] = part[rows_of(sub), :]

    loads[3].wait()
    loads[4].wait()
    padded = phase.shape[1]
    count = angle.shape[1]
    pick = lax.broadcasted_iota(jnp.int32, (padded, count), 1) == (
        lax.broadcasted_iota(jnp.int32, (padded, count), 0) + group * cones
    )
    polar = jnp.sum(jnp.where(pick, angle[0:1, :], 0.0), 1, keepdims=True)
    azimuth = jnp.sum(jnp.where(pick, angle[1:2, :], 0.0), 1, keepdims=True)
    sin_polar = jnp.sin(polar)
    argument = (
        (sin_polar * jnp.cos(azimuth)) * lane[0:1, :]
        + (sin_polar * jnp.sin(azimuth)) * lane[1:2, :]
        + jnp.cos(polar) * lane[2:3, :]
    )
    cosine, sine = jnp.cos(argument), jnp.sin(argument)
    sign = lane[3:4, :]
    phase[0] = cosine
    phase[1] = sine * sign
    phase[2] = 1.0 - 2.0 * sine * sine
    phase[3] = 2.0 * sine * cosine * sign
    loads[5].wait()
    loads[6].wait()

    def forward(index, e):
        there = half * blks + index
        return pltpu.make_async_remote_copy(
            src_ref=low.at[there],
            dst_ref=low.at[there],
            send_sem=send2.at[index, e],
            recv_sem=recv2.at[index, e],
            device_id=half_peer(e),
            device_id_type=MESH,
        )

    for step in range(blks):
        for t in range(subs):
            d = step * subs + t
            if d:
                copy(d).wait_recv()
        there = lax.rem(blk + (blks - step) % blks, blks)
        total = functools.reduce(jnp.add, [got[there, t] for t in range(subs)])
        low[half * blks + there] = total
        if step == 0:
            low_out[...] = total
        each(halves, lambda e: forward(there, e).start())
    def widen(value):
        fill = padded - cones
        if fill:
            value = jnp.concatenate([value, jnp.zeros((fill, value.shape[1]), value.dtype)], 0)
        return value.astype(F32)

    keep3 = widen(need3[...])
    lanes4 = need4.shape[1]
    diagonal = lax.broadcasted_iota(jnp.int32, (padded, lanes4), 0) == lax.broadcasted_iota(
        jnp.int32, (padded, lanes4), 1
    )

    def product(pieces):
        rows_in = pieces[0].shape[0]
        acc = None
        for t in range(OCT // 2):
            tile = split_rows(jnp.concatenate(pieces[2 * t : 2 * t + 2], 1))
            term = jnp.dot(tile, weight[2 * width * t : 2 * width * (t + 1), :], preferred_element_type=F32)
            acc = term if acc is None else acc + term
        return fold(acc, rows_in, width)

    def level_three(first):
        size = min(blks, OCT)
        for start in range(0, blks, size):
            boxes = [low[first + start + g] for g in range(size)]
            turned = [pltpu.roll(box, width // 2, 1) for box in boxes]
            pieces = []
            for o in range(OCT):
                lanes = slice(o * width, (o + 1) * width)
                cos_o, sin_o = phase[0, :, lanes], phase[1, :, lanes]
                pieces.append(
                    jnp.concatenate(
                        [cos_o * boxes[g][o : o + 1, :] + sin_o * turned[g][o : o + 1, :] for g in range(size)], 0
                    )
                )
            result = product(pieces)
            for g in range(size):
                three[first + start + g] = result[g * padded : (g + 1) * padded]

    level_three(half * blks)
    for step in range(blks):
        each(halves, lambda e: forward(lax.rem(blk + step, blks), e).wait_recv())
    for e in range(1, halves):
        level_three(lax.rem(half + e, halves) * blks)

    for q in range(groups // OCT):
        pieces = []
        for o in range(OCT):
            lanes = slice(o * width, (o + 1) * width)
            column = q * OCT + o
            box = three[column] * keep3[:, column : column + 1]
            pieces.append(phase[2, :, lanes] * box + phase[3, :, lanes] * pltpu.roll(box, width // 2, 1))
        keep4 = jnp.sum(jnp.where(diagonal, need4[q : q + 1, :].astype(F32), 0.0), 1, keepdims=True)
        four = product(pieces) * keep4
        cone_out[:, q, :] = four[:cones]

    each(blks * subs, lambda d: copy(d).wait_send())
    for step in range(blks):
        each(halves, lambda e: forward(lax.rem(blk + step, blks), e).wait_send())


def put_out(low_ref, cone_ref, low_out, cone_out, sems):
    copies = [
        pltpu.make_async_copy(low_ref, low_out, sems.at[0]),
        pltpu.make_async_copy(cone_ref, cone_out, sems.at[1]),
    ]
    for copy in copies:
        copy.start()
    for copy in copies:
        copy.wait()


def solution(mesh):
    halves, blks, subs = mesh.shape["half"], mesh.shape["blk"], mesh.shape["sub"]
    groups = halves * blks

    def local(leaf, occupied, angles, need3, need4):
        rows, width = leaf.shape
        pairs = rows // (2 * OCT)
        per_sub = pairs // subs
        cones = need3.shape[0]
        padded = -(-cones // 8) * 8
        assert per_sub == OCT and need3.shape[1] == groups
        weight = jnp.asarray(weight_table(ORDER))
        lane = jnp.asarray(lane_table(ORDER))
        occupied = occupied.reshape(rows // 128, 128)
        need4 = need4.T
        vmem = pl.BlockSpec(memory_space=pltpu.VMEM)
        anywhere = pl.BlockSpec(memory_space=pl.ANY)
        results = pl.pallas_call(
            functools.partial(kernel, halves, blks, subs, cones),
            out_shape=(
                pltpu.VMEM((per_sub, width), F32),
                pltpu.VMEM((cones, groups // OCT, width), F32),
            ),
            in_specs=[anywhere] * 7,
            out_specs=(vmem, vmem),
            scratch_shapes=[
                pltpu.VMEM(leaf.shape, F32),
                pltpu.VMEM(occupied.shape, jnp.int32),
                pltpu.VMEM(angles.shape, F32),
                pltpu.VMEM(need3.shape, jnp.int32),
                pltpu.VMEM(need4.shape, jnp.int32),
                pltpu.VMEM(weight.shape, BF16),
                pltpu.VMEM(lane.shape, F32),
                pltpu.VMEM((pairs, width), F32),
                pltpu.VMEM((blks, subs, per_sub, width), F32),
                pltpu.VMEM((groups, per_sub, width), F32),
                pltpu.VMEM((groups, padded, width), F32),
                pltpu.VMEM((4, padded, OCT * width), F32),
                pltpu.SemaphoreType.DMA((7,)),
                pltpu.SemaphoreType.DMA((blks * subs,)),
                pltpu.SemaphoreType.DMA((blks * subs,)),
                pltpu.SemaphoreType.DMA((blks, halves)),
                pltpu.SemaphoreType.DMA((blks, halves)),
            ],
            compiler_params=pltpu.CompilerParams(collective_id=0, has_side_effects=True),
            name="upward",
        )(leaf, occupied, angles, need3, need4, weight, lane)
        results = [pltpu.with_memory_space_constraint(value, pltpu.VMEM) for value in results]
        return pl.pallas_call(
            put_out,
            out_shape=[jax.ShapeDtypeStruct(value.shape, F32) for value in results],
            in_specs=[vmem] * 2,
            out_specs=[pl.BlockSpec(memory_space=pltpu.HBM)] * 2,
            scratch_shapes=[pltpu.SemaphoreType.DMA((2,))],
            name="put_out",
        )(*results)

    return jax.shard_map(
        local,
        mesh=mesh,
        in_specs=(
            P(("half", "blk", "sub"), None),
            P(("half", "blk", "sub")),
            P(),
            P(("half", "blk"), "sub"),
            P(("half", "blk"), "sub"),
        ),
        out_specs=(P(("half", "blk", "sub"), None), P(("half", "blk"), "sub", None)),
        check_vma=False,
    )
```

profile of v0, /device:TPU:1, one launch (start us, length us, event | category | flops | bytes accessed | tf_op | source)
XLA Modules:
  0.0 13.4 jit_solution(3872851338590189838)
XLA Ops:
  0.6 12.1 %upward.1 = (f32[8,128]{1,0:T(8,128)S(1)}, f32[6,1,128]{2,1,0:T(1,128)S(1)}) custom-call(f32[512,128]{1,0:T(8,128)} %leaf_hbm.1, s32[4,128]{1,0:T(4,128)} %bitcast.2, f32[2,48]{1,0:T(2,128)} %angle_hbm.1, s32[6,8]{1,0:T(8,128)} %need3_hbm.1, s32[1,6]{1,0:T(1,128)} %bitcast.3, bf16[1024,256]{1,0:T(8,128)(2,1)} %constant.4.clone.weight_hbm, ...), custom_call_target="tpu_custom_call" | custom-call | tf_op jit(solution)/shard_map/upward/pallas_call | solution.py:299
  12.7 0.6 %put_out.1 = (f32[8,128]{1,0:T(8,128)}, f32[6,1,128]{2,1,0:T(1,128)}) custom-call(f32[8,128]{1,0:T(8,128)S(1)} %get-tuple-element.4.low_ref, f32[6,1,128]{2,1,0:T(1,128)S(1)} %get-tuple-element.5.cone_ref), custom_call_target="tpu_custom_call" | custom-call | tf_op jit(solution)/shard_map/put_out/pallas_call | solution.py:330
where the time goes:
time: 13.5 us; the launch traced here: 13.4 us
  Pallas kernels  12.7 us (94%)
  between operations  0.64 us (5%)
    pallas_call x1, Pallas kernels, local(): pl.pallas_call(functools.partial(kernel, halves, blks, subs, cones), out_...  12.1 us
    pallas_call x1, Pallas kernels, local(): pl.pallas_call(put_out, out_shape=[jax.ShapeDtypeStruct(value.shape, F32)...  0.61 us

commit v1 on v0

--- a/solution.py
+++ b/solution.py
@@ -59,12 +59,12 @@
     return np.concatenate([offsets, sign[None]], 0).astype(np.float32)
 
 
-def each(count, body):
-    if count <= 64:
-        for d in range(1, count):
+def each(start, count, body):
+    if count - start <= 64:
+        for d in range(start, count):
             body(d)
     else:
-        lax.fori_loop(1, count, lambda d, c: (body(d), c)[1], 0)
+        lax.fori_loop(start, count, lambda d, c: (body(d), c)[1], 0)
 
 
 def split_rows(value):
@@ -81,7 +81,7 @@
     halves, blks, subs, cones,
     leaf_hbm, occ_hbm, angle_hbm, need3_hbm, need4_hbm, weight_hbm, lane_hbm,
     low_out, cone_out,
-    leaf, occ, angle, need3, need4, weight, lane, part, got, low, three, phase,
+    leaf, occ, angle, need3, need4, weight, lane, part, got, mine, theirs, three, phase,
     in_sem, send, recv, send2, recv2,
 ):
     groups = halves * blks
@@ -101,20 +101,22 @@
     for load in loads:
         load.start()
 
+    other = halves - 1 - half
+
+    def blk_of(j):
+        return lax.rem(j + blks - 1 - blk, blks)
+
+    def sub_of(t):
+        return lax.rem(t + subs - 1 - sub, subs)
+
     def peer(d):
-        there = lax.rem(blk + d // subs, blks)
-        return {"blk": there, "sub": lax.rem(sub + lax.rem(d, subs), subs)}
-
-    def half_peer(e):
-        return {"half": lax.rem(half + e, halves)}
+        return {"half": other, "blk": blk_of(d // subs), "sub": sub_of(lax.rem(d, subs))}
 
     barrier = pltpu.get_barrier_semaphore()
-
-    def greet(target):
-        pl.semaphore_signal(barrier, inc=1, device_id=target, device_id_type=MESH)
-
-    each(halves, lambda e: greet(half_peer(e)))
-    each(blks * subs, lambda d: greet(peer(d)))
+    each(
+        0, blks * subs,
+        lambda d: pl.semaphore_signal(barrier, inc=1, device_id=peer(d), device_id_type=MESH),
+    )
 
     loads[0].wait()
     loads[1].wait()
@@ -140,26 +142,23 @@
         acc = term if acc is None else acc + term
     one = fold(acc, 2 * pairs, width)
     tile = jnp.concatenate([one[:pairs], one[pairs:]], 1)
-    mine = weight[pl.ds(pl.multiple_of(sub * 2 * width, 2 * width), 2 * width), :]
-    part[...] = fold(jnp.dot(split_rows(tile), mine, preferred_element_type=F32), pairs, width)
-
-    pl.semaphore_wait(barrier, blks * subs + halves - 2)
-
-    def rows_of(index):
-        return pl.ds(pl.multiple_of(index * per_sub, 8), per_sub)
+    ours = weight[pl.ds(pl.multiple_of(sub * 2 * width, 2 * width), 2 * width), :]
+    part[...] = fold(jnp.dot(split_rows(tile), ours, preferred_element_type=F32), pairs, width)
+
+    pl.semaphore_wait(barrier, blks * subs)
 
     def copy(d):
+        there = peer(d)
         return pltpu.make_async_remote_copy(
-            src_ref=part.at[rows_of(lax.rem(sub + lax.rem(d, subs), subs))],
-            dst_ref=got.at[blk, sub],
-            send_sem=send.at[d],
-            recv_sem=recv.at[d],
-            device_id=peer(d),
+            src_ref=part.at[pl.ds(pl.multiple_of(there["sub"] * per_sub, 8), per_sub)],
+            dst_ref=got.at[d // subs * subs + sub],
+            send_sem=send.at[0],
+            recv_sem=recv.at[jnp.minimum(d // subs, 1)],
+            device_id=there,
             device_id_type=MESH,
         )
 
-    each(blks * subs, lambda d: copy(d).start())
-    got[blk, sub] = part[rows_of(sub), :]
+    each(0, blks * subs, lambda d: copy(d).start())
 
     loads[3].wait()
     loads[4].wait()
@@ -185,28 +184,6 @@
     loads[5].wait()
     loads[6].wait()
 
-    def forward(index, e):
-        there = half * blks + index
-        return pltpu.make_async_remote_copy(
-            src_ref=low.at[there],
-            dst_ref=low.at[there],
-            send_sem=send2.at[index, e],
-            recv_sem=recv2.at[index, e],
-            device_id=half_peer(e),
-            device_id_type=MESH,
-        )
-
-    for step in range(blks):
-        for t in range(subs):
-            d = step * subs + t
-            if d:
-                copy(d).wait_recv()
-        there = lax.rem(blk + (blks - step) % blks, blks)
-        total = functools.reduce(jnp.add, [got[there, t] for t in range(subs)])
-        low[half * blks + there] = total
-        if step == 0:
-            low_out[...] = total
-        each(halves, lambda e: forward(there, e).start())
     def widen(value):
         fill = padded - cones
         if fill:
@@ -228,29 +205,59 @@
             acc = term if acc is None else acc + term
         return fold(acc, rows_in, width)
 
-    def level_three(first):
-        size = min(blks, OCT)
-        for start in range(0, blks, size):
-            boxes = [low[first + start + g] for g in range(size)]
-            turned = [pltpu.roll(box, width // 2, 1) for box in boxes]
-            pieces = []
-            for o in range(OCT):
-                lanes = slice(o * width, (o + 1) * width)
-                cos_o, sin_o = phase[0, :, lanes], phase[1, :, lanes]
-                pieces.append(
-                    jnp.concatenate(
-                        [cos_o * boxes[g][o : o + 1, :] + sin_o * turned[g][o : o + 1, :] for g in range(size)], 0
-                    )
+    def level_three(start, size):
+        named = [
+            (box, first + blk_of(j))
+            for j in range(start, start + size)
+            for box, first in ((mine[j], other * blks), (theirs[j], half * blks))
+        ]
+        boxes = [box for box, _ in named]
+        turned = [pltpu.roll(box, width // 2, 1) for box in boxes]
+        pieces = []
+        for o in range(OCT):
+            lanes = slice(o * width, (o + 1) * width)
+            cos_o, sin_o = phase[0, :, lanes], phase[1, :, lanes]
+            pieces.append(
+                jnp.concatenate(
+                    [cos_o * box[o : o + 1, :] + sin_o * turn[o : o + 1, :] for box, turn in zip(boxes, turned)], 0
                 )
-            result = product(pieces)
-            for g in range(size):
-                three[first + start + g] = result[g * padded : (g + 1) * padded]
-
-    level_three(half * blks)
-    for step in range(blks):
-        each(halves, lambda e: forward(lax.rem(blk + step, blks), e).wait_recv())
-    for e in range(1, halves):
-        level_three(lax.rem(half + e, halves) * blks)
+            )
+        result = product(pieces)
+        for g, (_, index) in enumerate(named):
+            three[index] = result[g * padded : (g + 1) * padded]
+
+    far, near = pl.ds(0, 1), pl.ds(1, blks - 1)
+
+    def landed(k):
+        slots = got.at[pl.ds(0, subs)] if k == 0 else got.at[pl.ds(subs, (blks - 1) * subs)]
+        return pltpu.make_async_copy(slots, slots, recv.at[k])
+
+    def total(j):
+        mine[j] = functools.reduce(jnp.add, [got[j * subs + t] for t in range(subs)])
+
+    def forward(k):
+        boxes = far if k == 0 else near
+        return pltpu.make_async_remote_copy(
+            src_ref=mine.at[boxes],
+            dst_ref=theirs.at[boxes],
+            send_sem=send2.at[0],
+            recv_sem=recv2.at[k],
+            device_id={"half": other},
+            device_id_type=MESH,
+        )
+
+    landed(1).wait()
+    each(1, blks, total)
+    forward(1).start()
+    landed(0).wait()
+    total(0)
+    forward(0).start()
+    forward(1).wait_recv()
+    for start in range(1, blks, 3):
+        level_three(start, min(3, blks - start))
+    forward(0).wait_recv()
+    low_out[...] = theirs[lax.rem(2 * blk + 1, blks)]
+    level_three(0, 1)
 
     for q in range(groups // OCT):
         pieces = []
@@ -263,9 +270,8 @@
         four = product(pieces) * keep4
         cone_out[:, q, :] = four[:cones]
 
-    each(blks * subs, lambda d: copy(d).wait_send())
-    for step in range(blks):
-        each(halves, lambda e: forward(lax.rem(blk + step, blks), e).wait_send())
+    pltpu.make_async_copy(got, got, send.at[0]).wait()
+    pltpu.make_async_copy(mine, mine, send2.at[0]).wait()
 
 
 def put_out(low_ref, cone_ref, low_out, cone_out, sems):
@@ -289,7 +295,7 @@
         per_sub = pairs // subs
         cones = need3.shape[0]
         padded = -(-cones // 8) * 8
-        assert per_sub == OCT and need3.shape[1] == groups
+        assert per_sub == OCT and need3.shape[1] == groups and halves == 2
         weight = jnp.asarray(weight_table(ORDER))
         lane = jnp.asarray(lane_table(ORDER))
         occupied = occupied.reshape(rows // 128, 128)
@@ -313,15 +319,16 @@
                 pltpu.VMEM(weight.shape, BF16),
                 pltpu.VMEM(lane.shape, F32),
                 pltpu.VMEM((pairs, width), F32),
-                pltpu.VMEM((blks, subs, per_sub, width), F32),
-                pltpu.VMEM((groups, per_sub, width), F32),
+                pltpu.VMEM((blks * subs, per_sub, width), F32),
+                pltpu.VMEM((blks, per_sub, width), F32),
+                pltpu.VMEM((blks, per_sub, width), F32),
                 pltpu.VMEM((groups, padded, width), F32),
                 pltpu.VMEM((4, padded, OCT * width), F32),
                 pltpu.SemaphoreType.DMA((7,)),
-                pltpu.SemaphoreType.DMA((blks * subs,)),
-                pltpu.SemaphoreType.DMA((blks * subs,)),
-                pltpu.SemaphoreType.DMA((blks, halves)),
-                pltpu.SemaphoreType.DMA((blks, halves)),
+                pltpu.SemaphoreType.DMA((1,)),
+                pltpu.SemaphoreType.DMA((2,)),
+                pltpu.SemaphoreType.DMA((1,)),
+                pltpu.SemaphoreType.DMA((2,)),
             ],
             compiler_params=pltpu.CompilerParams(collective_id=0, has_side_effects=True),
             name="upward",

time: 13.5 us -> 13.3 us (0.985)
  the two profiles are of different devices: /device:TPU:1 before, /device:TPU:0 now
where the time goes in v1:
time: 13.3 us; the launch traced here: 13.1 us
  Pallas kernels  12.5 us (94%)
  between operations  0.64 us (5%)
    pallas_call x1, Pallas kernels, local(): pl.pallas_call(functools.partial(kernel, halves, blks, subs, cones), out_...  11.8 us
    pallas_call x1, Pallas kernels, local(): pl.pallas_call(put_out, out_shape=[jax.ShapeDtypeStruct(value.shape, F32)...  0.61 us

profile of v1, /device:TPU:0, one launch (start us, length us, event | category | flops | bytes accessed | tf_op | source)
XLA Modules:
  0.0 13.1 jit_solution(14477421440182073915)
XLA Ops:
  0.6 11.8 %upward.1 = (f32[8,128]{1,0:T(8,128)S(1)}, f32[6,1,128]{2,1,0:T(1,128)S(1)}) custom-call(f32[512,128]{1,0:T(8,128)} %leaf_hbm.1, s32[4,128]{1,0:T(4,128)} %bitcast.2, f32[2,48]{1,0:T(2,128)} %angle_hbm.1, s32[6,8]{1,0:T(8,128)} %need3_hbm.1, s32[1,6]{1,0:T(1,128)} %bitcast.3, bf16[1024,256]{1,0:T(8,128)(2,1)} %constant.4.clone.weight_hbm, ...), custom_call_target="tpu_custom_call" | custom-call | tf_op jit(solution)/shard_map/upward/pallas_call | solution.py:305
  12.5 0.6 %put_out.1 = (f32[8,128]{1,0:T(8,128)}, f32[6,1,128]{2,1,0:T(1,128)}) custom-call(f32[8,128]{1,0:T(8,128)S(1)} %get-tuple-element.4.low_ref, f32[6,1,128]{2,1,0:T(1,128)S(1)} %get-tuple-element.5.cone_ref), custom_call_target="tpu_custom_call" | custom-call | tf_op jit(solution)/shard_map/put_out/pallas_call | solution.py:337

commit v2 on v1

--- a/solution.py
+++ b/solution.py
@@ -1,5 +1,6 @@
 import functools
 import math
+import operator
 
 import jax
 import jax.numpy as jnp
@@ -82,7 +83,7 @@
     leaf_hbm, occ_hbm, angle_hbm, need3_hbm, need4_hbm, weight_hbm, lane_hbm,
     low_out, cone_out,
     leaf, occ, angle, need3, need4, weight, lane, part, got, mine, theirs, three, phase,
-    in_sem, send, recv, send2, recv2,
+    in_sem, send, recv, send2, recv2, ready,
 ):
     groups = halves * blks
     half, blk, sub = lax.axis_index("half"), lax.axis_index("blk"), lax.axis_index("sub")
@@ -112,11 +113,19 @@
     def peer(d):
         return {"half": other, "blk": blk_of(d // subs), "sub": sub_of(lax.rem(d, subs))}
 
+    def planes(wanted, act):
+        def plane(j):
+            @pl.when(wanted(blk_of(j), blk))
+            def _():
+                each(0, subs, lambda t: act(j * subs + t))
+
+        each(0, blks, plane)
+
+    def greet(semaphore):
+        return lambda d: pl.semaphore_signal(semaphore, inc=1, device_id=peer(d), device_id_type=MESH)
+
     barrier = pltpu.get_barrier_semaphore()
-    each(
-        0, blks * subs,
-        lambda d: pl.semaphore_signal(barrier, inc=1, device_id=peer(d), device_id_type=MESH),
-    )
+    planes(operator.ge, greet(barrier))
 
     loads[0].wait()
     loads[1].wait()
@@ -145,7 +154,7 @@
     ours = weight[pl.ds(pl.multiple_of(sub * 2 * width, 2 * width), 2 * width), :]
     part[...] = fold(jnp.dot(split_rows(tile), ours, preferred_element_type=F32), pairs, width)
 
-    pl.semaphore_wait(barrier, blks * subs)
+    pl.semaphore_wait(barrier, (blk + 1) * subs)
 
     def copy(d):
         there = peer(d)
@@ -158,7 +167,8 @@
             device_id_type=MESH,
         )
 
-    each(0, blks * subs, lambda d: copy(d).start())
+    planes(operator.le, lambda d: copy(d).start())
+    planes(operator.lt, lambda d: greet(ready.at[d // subs])(d))
 
     loads[3].wait()
     loads[4].wait()
@@ -225,6 +235,15 @@
         result = product(pieces)
         for g, (_, index) in enumerate(named):
             three[index] = result[g * padded : (g + 1) * padded]
+
+    def outward(k):
+        @pl.when(blk + k < blks)
+        def _():
+            j = lax.rem(2 * blk + k + 1, blks)
+            pl.semaphore_wait(ready.at[j], subs)
+            each(0, subs, lambda t: copy(j * subs + t).start())
+
+    each(1, blks, outward)
 
     far, near = pl.ds(0, 1), pl.ds(1, blks - 1)
 
@@ -329,6 +348,7 @@
                 pltpu.SemaphoreType.DMA((2,)),
                 pltpu.SemaphoreType.DMA((1,)),
                 pltpu.SemaphoreType.DMA((2,)),
+                pltpu.SemaphoreType.REGULAR((blks,)),
             ],
             compiler_params=pltpu.CompilerParams(collective_id=0, has_side_effects=True),
             name="upward",

time: 13.3 us -> 12.9 us (0.970)
  Pallas kernels: 12.5 us -> 12.1 us
    pallas_call x1, Pallas kernels: 11.8 us -> 11.4 us  [local(): pl.pallas_call(functools.partial(kernel, halves, blks, subs, cones), out_...]
where the time goes in v2:
time: 12.9 us; the launch traced here: 12.7 us
  Pallas kernels  12.1 us (94%)
  between operations  0.64 us (5%)
    pallas_call x1, Pallas kernels, local(): pl.pallas_call(functools.partial(kernel, halves, blks, subs, cones), out_...  11.4 us
    pallas_call x1, Pallas kernels, local(): pl.pallas_call(put_out, out_shape=[jax.ShapeDtypeStruct(value.shape, F32)...  0.61 us

profile of v2, /device:TPU:0, one launch (start us, length us, event | category | flops | bytes accessed | tf_op | source)
XLA Modules:
  0.0 12.7 jit_solution(15790882420611546598)
XLA Ops:
  0.6 11.4 %upward.1 = (f32[8,128]{1,0:T(8,128)S(1)}, f32[6,1,128]{2,1,0:T(1,128)S(1)}) custom-call(f32[512,128]{1,0:T(8,128)} %leaf_hbm.1, s32[4,128]{1,0:T(4,128)} %bitcast.2, f32[2,48]{1,0:T(2,128)} %angle_hbm.1, s32[6,8]{1,0:T(8,128)} %need3_hbm.1, s32[1,6]{1,0:T(1,128)} %bitcast.3, bf16[1024,256]{1,0:T(8,128)(2,1)} %constant.4.clone.weight_hbm, ...), custom_call_target="tpu_custom_call" | custom-call | tf_op jit(solution)/shard_map/upward/pallas_call | solution.py:324
  12.1 0.6 %put_out.1 = (f32[8,128]{1,0:T(8,128)}, f32[6,1,128]{2,1,0:T(1,128)}) custom-call(f32[8,128]{1,0:T(8,128)S(1)} %get-tuple-element.4.low_ref, f32[6,1,128]{2,1,0:T(1,128)S(1)} %get-tuple-element.5.cone_ref), custom_call_target="tpu_custom_call" | custom-call | tf_op jit(solution)/shard_map/put_out/pallas_call | solution.py:357

commit v3 on v2

v3 whole, which is shorter than its diff:
```python
import functools
import math
import operator

import jax
import jax.numpy as jnp
import numpy as np
from jax import lax
from jax.experimental import pallas as pl
from jax.experimental.pallas import tpu as pltpu
from jax.sharding import PartitionSpec as P

MESH = pl.DeviceIdType.MESH
F32, BF16 = jnp.float32, jnp.bfloat16
ORDER = 4
OCT = 8
NEAR = 1.5


def octant_signs():
    octant = np.arange(OCT)
    return np.stack([octant // 4 % 2, octant // 2 % 2, octant % 2], -1) * 2.0 - 1.0


def chebyshev_points(per_axis):
    return np.cos((2.0 * np.arange(per_axis) + 1.0) * math.pi / (2.0 * per_axis))


def axis_table():
    points = chebyshev_points(ORDER)
    degree = np.arange(1, ORDER)
    shifted = (points[None, :] + np.array([-1.0, 1.0])[:, None]) / 2.0
    here = np.cos(degree[None, :] * np.arccos(points)[:, None])
    there = np.cos(degree * np.arccos(shifted)[:, :, None])
    return 1.0 / ORDER + 2.0 / ORDER * np.einsum("mk,bnk->bnm", here, there)


def each(start, count, body):
    if count - start <= 64:
        for d in range(start, count):
            body(d)
    else:
        lax.fori_loop(start, count, lambda d, c: (body(d), c)[1], 0)


def split_rows(value):
    high = value.astype(BF16)
    low = (value - high.astype(F32)).astype(BF16)
    return jnp.concatenate([high, low], 0)


def fold(acc, rows, width):
    return (acc[:rows, :width] + acc[rows:, :width]) + (acc[:rows, width:] + acc[rows:, width:])


def choose(digit, values):
    return jnp.where(
        digit < 2, jnp.where(digit == 0, values[0], values[1]), jnp.where(digit == 2, values[2], values[3])
    )


def digit_of(index, place):
    return lax.rem(index // place, ORDER)


def build(table, then, bits, nodes, place):
    tile = (8, 2 * nodes)
    row, lane = lax.broadcasted_iota(jnp.int32, tile, 0), lax.broadcasted_iota(jnp.int32, tile, 1)

    def along(first, bit, i, stride):
        if bit is None:
            values = [float(table[first, i, j]) for j in range(ORDER)]
        elif isinstance(bit, int):
            values = [float(then[first, bit, i, j]) for j in range(ORDER)]
        else:
            values = [
                jnp.where(bit == 0, float(then[first, 0, i, j]), float(then[first, 1, i, j]))
                for j in range(ORDER)
            ]
        return choose(digit_of(lane, stride), values)

    bit_x, bit_y, thirds = bits
    xs = [[along(b, bit_x, i, ORDER * ORDER) for i in range(ORDER)] for b in range(2)]
    ys = [
        [jnp.where(row < ORDER, along(b, bit_y, 2 * i, ORDER), along(b, bit_y, 2 * i + 1, ORDER)) for i in range(2)]
        for b in range(2)
    ]
    zs = [
        [choose(digit_of(row, 1), [along(b, bit, i, 1) for i in range(ORDER)]) for b in range(2)] for bit in thirds
    ]
    real = lane < nodes
    for o in range(OCT):
        plane = [xs[o // 4][i // 2] * ys[o // 2 % 2][i % 2] for i in range(nodes // 8)]
        for r, third in enumerate(zs):
            block = [value * third[o % 2] for value in plane]
            wide = jnp.concatenate(
                [jnp.where(real, value, 0.0) for value in block] + [jnp.where(real, 0.0, value) for value in block], 0
            )
            high = wide.astype(BF16)
            low = (wide - high.astype(F32)).astype(BF16)
            place[pl.ds((r * OCT + o) * 2 * nodes, 2 * nodes), :] = jnp.concatenate([high, low], 1)


def product(tiles, weights):
    rows, width = tiles[0].shape
    sums = [None, None]
    for t, (tile, block) in enumerate(zip(tiles, weights)):
        term = jnp.dot(split_rows(tile), block, preferred_element_type=F32)
        sums[t % 2] = term if sums[t % 2] is None else sums[t % 2] + term
    halves = [fold(value, rows, width // 2) for value in sums if value is not None]
    return functools.reduce(jnp.add, halves)


def kernel(
    halves, blks, subs, cones,
    leaf_hbm, occ_hbm, angle_hbm, need3_hbm, need4_hbm,
    low_out, cone_out,
    leaf, occ, keep, angle, need3, need4, both, weight, part, got, mine, theirs, near, far, four,
    in_sem, send, recv, send2, recv2, ready,
):
    groups = halves * blks
    half, blk, sub = lax.axis_index("half"), lax.axis_index("blk"), lax.axis_index("sub")
    group = half * blks + blk
    pairs, family, width = leaf_hbm.shape
    nodes = width // 2
    per_sub = pairs // subs

    pltpu.make_async_copy(occ_hbm, occ, in_sem.at[0]).start()
    for q in range(family):
        pltpu.make_async_copy(leaf_hbm.at[:, q], leaf.at[pl.ds(q * pairs, pairs)], in_sem.at[1]).start()
    loads = [
        pltpu.make_async_copy(src, dst, in_sem.at[2 + i])
        for i, (src, dst) in enumerate([(angle_hbm, angle), (need3_hbm, need3), (need4_hbm, need4)])
    ]
    for load in loads:
        load.start()

    other = halves - 1 - half

    def blk_of(j):
        return lax.rem(j + blks - 1 - blk, blks)

    def sub_of(t):
        return lax.rem(t + subs - 1 - sub, subs)

    def peer(d):
        return {"half": other, "blk": blk_of(d // subs), "sub": sub_of(lax.rem(d, subs))}

    def planes(wanted, act):
        def plane(j):
            @pl.when(wanted(blk_of(j), blk))
            def _():
                each(0, subs, lambda t: act(j * subs + t))

        each(0, blks, plane)

    def greet(semaphore):
        return lambda d: pl.semaphore_signal(semaphore, inc=1, device_id=peer(d), device_id_type=MESH)

    barrier = pltpu.get_barrier_semaphore()
    planes(operator.ge, greet(barrier))

    table = axis_table()
    then = np.einsum("bij,qjk->bqik", table, table)
    build(table, then, (lax.rem(sub // 2, 2), lax.rem(sub, 2), (0, 1)), nodes, both)

    pltpu.make_async_copy(occ_hbm, occ, in_sem.at[0]).wait()
    columns = jnp.transpose(occ[...].astype(F32))
    for i in range(pairs * family // 8):
        rows8 = columns[8 * (i % 16) : 8 * (i % 16) + 8, i // 16 : i // 16 + 1]
        keep[pl.ds(i % 2 * 8 * pairs + i // 2, 8, stride=pairs), :] = jnp.broadcast_to(rows8, (8, width))
    pltpu.make_async_copy(leaf, leaf, in_sem.at[1]).wait()
    masked = [leaf[q * pairs : (q + 1) * pairs, :] * keep[q * pairs : (q + 1) * pairs, :] for q in range(family)]
    part[...] = product(
        [jnp.concatenate(masked[2 * t : 2 * t + 2], 1) for t in range(family // 2)],
        [both[2 * width * t : 2 * width * (t + 1), :] for t in range(family // 2)],
    )

    pl.semaphore_wait(barrier, (blk + 1) * subs)

    def copy(d):
        there = peer(d)
        return pltpu.make_async_remote_copy(
            src_ref=part.at[pl.ds(pl.multiple_of(there["sub"] * per_sub, 8), per_sub)],
            dst_ref=got.at[d // subs * subs + sub],
            send_sem=send.at[0],
            recv_sem=recv.at[jnp.minimum(d // subs, 1)],
            device_id=there,
            device_id_type=MESH,
        )

    planes(operator.le, lambda d: copy(d).start())
    planes(operator.lt, lambda d: greet(ready.at[d // subs])(d))

    build(table, then, (None, None, (None,)), nodes, weight)

    loads[0].wait()
    padded = near.shape[2]
    count = angle.shape[1]
    pick = lax.broadcasted_iota(jnp.int32, (padded, count), 1) == (
        lax.broadcasted_iota(jnp.int32, (padded, count), 0) + group * cones
    )
    polar = jnp.sum(jnp.where(pick, angle[0:1, :], 0.0), 1, keepdims=True)
    azimuth = jnp.sum(jnp.where(pick, angle[1:2, :], 0.0), 1, keepdims=True)
    sin_polar = jnp.sin(polar)
    direction = [sin_polar * jnp.cos(azimuth), sin_polar * jnp.sin(azimuth), jnp.cos(polar)]
    lane = lax.broadcasted_iota(jnp.int32, (padded, width), 1)
    points = [float(value) for value in chebyshev_points(ORDER)]
    places = [choose(digit_of(lane, ORDER**power), points) for power in (2, 1, 0)]
    sign = jnp.where(lane < nodes, -1.0, 1.0)
    for load in loads[1:]:
        load.wait()

    def widen(value):
        fill = padded - cones
        if fill:
            value = jnp.concatenate([value, jnp.zeros((fill, value.shape[1]), value.dtype)], 0)
        return value.astype(F32)

    keep3 = widen(need3[...])
    signs = octant_signs()
    for o in range(OCT):
        argument = sum(
            axis * (place + float(signs[o, d])) for d, (axis, place) in enumerate(zip(direction, places))
        ) * -NEAR
        cosine, sine = jnp.cos(argument), jnp.sin(argument)
        near[0, o] = cosine
        near[1, o] = sine * sign
        for g in range(o, groups, OCT):
            kept = keep3[:, g : g + 1]
            far[0, g] = (1.0 - 2.0 * sine * sine) * kept
            far[1, g] = 2.0 * sine * cosine * sign * kept
    lanes4 = need4.shape[1]
    diagonal = lax.broadcasted_iota(jnp.int32, (padded, lanes4), 0) == lax.broadcasted_iota(
        jnp.int32, (padded, lanes4), 1
    )
    keep4 = [
        jnp.sum(jnp.where(diagonal, need4[q : q + 1, :].astype(F32), 0.0), 1, keepdims=True)
        for q in range(groups // OCT)
    ]

    def outward(k):
        @pl.when(blk + k < blks)
        def _():
            j = lax.rem(2 * blk + k + 1, blks)
            pl.semaphore_wait(ready.at[j], subs)
            each(0, subs, lambda t: copy(j * subs + t).start())

    each(1, blks, outward)

    def level_three(start, size):
        boxes = [box for j in range(start, start + size) for box in (mine[j], theirs[j])]
        turned = [pltpu.roll(box, nodes, 1) for box in boxes]
        pieces = [
            jnp.concatenate(
                [near[0, o] * box[o : o + 1, :] + near[1, o] * turn[o : o + 1, :] for box, turn in zip(boxes, turned)], 0
            )
            for o in range(OCT)
        ]
        result = product(
            [jnp.concatenate(pieces[2 * t : 2 * t + 2], 1) for t in range(OCT // 2)],
            [weight[2 * width * t : 2 * width * (t + 1), :] for t in range(OCT // 2)],
        )
        index = [first + blk_of(j) for j in range(start, start + size) for first in (other * blks, half * blks)]
        return [(g, result[i * padded : (i + 1) * padded]) for i, g in enumerate(index)]

    def rows_of(g, start, size):
        base = lax.rem(g, OCT) * width + start
        return weight[pl.ds(pl.multiple_of(base, nodes), size), :]

    def level_four(found):
        turned = [far[0, g] * box + far[1, g] * pltpu.roll(box, nodes, 1) for g, box in found]
        return product(
            [jnp.concatenate(turned[i : i + 2], 1) for i in range(0, len(found), 2)],
            [
                jnp.concatenate([rows_of(g, 0, width) for g, _ in found[i : i + 2]], 0)
                for i in range(0, len(found), 2)
            ],
        )

    def level_four_last(found):
        return product(
            [jnp.concatenate([far[0, g] * box, far[1, g] * -box], 1) for g, box in found],
            [
                jnp.concatenate([rows_of(g, 0, width), rows_of(g, nodes, nodes), rows_of(g, 0, nodes)], 0)
                for g, _ in found
            ],
        )

    last, rest = pl.ds(0, 1), pl.ds(1, blks - 1)

    def landed(k):
        slots = got.at[pl.ds(0, subs)] if k == 0 else got.at[pl.ds(subs, (blks - 1) * subs)]
        return pltpu.make_async_copy(slots, slots, recv.at[k])

    def total(j):
        mine[j] = functools.reduce(jnp.add, [got[j * subs + t] for t in range(subs)])

    def forward(k):
        boxes = last if k == 0 else rest
        return pltpu.make_async_remote_copy(
            src_ref=mine.at[boxes],
            dst_ref=theirs.at[boxes],
            send_sem=send2.at[0],
            recv_sem=recv2.at[k],
            device_id={"half": other},
            device_id_type=MESH,
        )

    landed(1).wait()
    each(1, blks, total)
    forward(1).start()
    landed(0).wait()
    total(0)
    forward(0).start()
    forward(1).wait_recv()
    single = groups == OCT
    if single:
        early = level_four(level_three(1, blks - 1))
    else:
        four[...] = jnp.zeros_like(four)
        for start in range(1, blks, 3):
            for g, box in level_three(start, min(3, blks - start)):
                four[g // OCT] += level_four_last([(g, box)])
    forward(0).wait_recv()
    low_out[...] = theirs[lax.rem(2 * blk + 1, blks)]
    if single:
        cone_out[:, 0, :] = ((early + level_four_last(level_three(0, 1))) * keep4[0])[:cones]
    else:
        for g, box in level_three(0, 1):
            four[g // OCT] += level_four_last([(g, box)])
        for q in range(groups // OCT):
            cone_out[:, q, :] = (four[q] * keep4[q])[:cones]

    pltpu.make_async_copy(got, got, send.at[0]).wait()
    pltpu.make_async_copy(mine, mine, send2.at[0]).wait()


def put_out(low_ref, cone_ref, low_out, cone_out, sems):
    copies = [
        pltpu.make_async_copy(low_ref, low_out, sems.at[0]),
        pltpu.make_async_copy(cone_ref, cone_out, sems.at[1]),
    ]
    for copy in copies:
        copy.start()
    for copy in copies:
        copy.wait()


def solution(mesh):
    halves, blks, subs = mesh.shape["half"], mesh.shape["blk"], mesh.shape["sub"]
    groups = halves * blks

    def local(leaf, occupied, angles, need3, need4):
        rows, width = leaf.shape
        family = 2 * OCT
        pairs = rows // family
        per_sub = pairs // subs
        cones = need3.shape[0]
        padded = -(-cones // 8) * 8
        assert per_sub == OCT and need3.shape[1] == groups and halves == 2 and subs * 2 == OCT
        assert width == 2 * ORDER**3 and blks % 2 == 0
        leaf = leaf.reshape(pairs, family, width)
        occupied = occupied.reshape(rows // 128, 128)
        need4 = need4.T
        vmem = pl.BlockSpec(memory_space=pltpu.VMEM)
        anywhere = pl.BlockSpec(memory_space=pl.ANY)
        results = pl.pallas_call(
            functools.partial(kernel, halves, blks, subs, cones),
            out_shape=(
                pltpu.VMEM((per_sub, width), F32),
                pltpu.VMEM((cones, groups // OCT, width), F32),
            ),
            in_specs=[anywhere] * 5,
            out_specs=(vmem, vmem),
            scratch_shapes=[
                pltpu.VMEM((rows, width), F32),
                pltpu.VMEM(occupied.shape, jnp.int32),
                pltpu.VMEM((rows, width), F32),
                pltpu.VMEM(angles.shape, F32),
                pltpu.VMEM(need3.shape, jnp.int32),
                pltpu.VMEM(need4.shape, jnp.int32),
                pltpu.VMEM((family * width, 2 * width), BF16),
                pltpu.VMEM((OCT * width, 2 * width), BF16),
                pltpu.VMEM((pairs, width), F32),
                pltpu.VMEM((blks * subs, per_sub, width), F32),
                pltpu.VMEM((blks, per_sub, width), F32),
                pltpu.VMEM((blks, per_sub, width), F32),
                pltpu.VMEM((2, OCT, padded, width), F32),
                pltpu.VMEM((2, groups, padded, width), F32),
                pltpu.VMEM((groups // OCT, padded, width), F32),
                pltpu.SemaphoreType.DMA((5,)),
                pltpu.SemaphoreType.DMA((1,)),
                pltpu.SemaphoreType.DMA((2,)),
                pltpu.SemaphoreType.DMA((1,)),
                pltpu.SemaphoreType.DMA((2,)),
                pltpu.SemaphoreType.REGULAR((blks,)),
            ],
            compiler_params=pltpu.CompilerParams(collective_id=0, has_side_effects=True),
            name="upward",
        )(leaf, occupied, angles, need3, need4)
        results = [pltpu.with_memory_space_constraint(value, pltpu.VMEM) for value in results]
        return pl.pallas_call(
            put_out,
            out_shape=[jax.ShapeDtypeStruct(value.shape, F32) for value in results],
            in_specs=[vmem] * 2,
            out_specs=[pl.BlockSpec(memory_space=pltpu.HBM)] * 2,
            scratch_shapes=[pltpu.SemaphoreType.DMA((2,))],
            name="put_out",
        )(*results)

    return jax.shard_map(
        local,
        mesh=mesh,
        in_specs=(
            P(("half", "blk", "sub"), None),
            P(("half", "blk", "sub")),
            P(),
            P(("half", "blk"), "sub"),
            P(("half", "blk"), "sub"),
        ),
        out_specs=(P(("half", "blk", "sub"), None), P(("half", "blk"), "sub", None)),
        check_vma=False,
    )
```

time: 12.9 us -> 12.3 us (0.953)
  Pallas kernels: 12.1 us -> 11.5 us
    pallas_call x1, Pallas kernels: 11.4 us -> 10.9 us  [local(): pl.pallas_call(functools.partial(kernel, halves, blks, subs, cones), out_...]
where the time goes in v3:
time: 12.3 us; the launch traced here: 12.1 us
  Pallas kernels  11.5 us (93%)
  between operations  0.64 us (5%)
    pallas_call x1, Pallas kernels, local(): pl.pallas_call(functools.partial(kernel, halves, blks, subs, cones), out_...  10.9 us
    pallas_call x1, Pallas kernels, local(): pl.pallas_call(put_out, out_shape=[jax.ShapeDtypeStruct(value.shape, F32)...  0.61 us

profile of v3, /device:TPU:0, one launch (start us, length us, event | category | flops | bytes accessed | tf_op | source)
XLA Modules:
  0.0 12.1 jit_solution(3184841673450364167)
XLA Ops:
  0.6 10.9 %upward.1 = (f32[8,128]{1,0:T(8,128)S(1)}, f32[6,1,128]{2,1,0:T(1,128)S(1)}) custom-call(f32[32,16,128]{2,1,0:T(8,128)} %bitcast.3, s32[4,128]{1,0:T(4,128)} %bitcast.4, f32[2,48]{1,0:T(2,128)} %angle_hbm.1, s32[6,8]{1,0:T(8,128)} %need3_hbm.1, s32[1,6]{1,0:T(1,128)} %bitcast.5), custom_call_target="tpu_custom_call" | custom-call | tf_op jit(solution)/shard_map/upward/pallas_call | solution.py:368
  11.5 0.6 %put_out.1 = (f32[8,128]{1,0:T(8,128)}, f32[6,1,128]{2,1,0:T(1,128)}) custom-call(f32[8,128]{1,0:T(8,128)S(1)} %get-tuple-element.4.low_ref, f32[6,1,128]{2,1,0:T(1,128)S(1)} %get-tuple-element.5.cone_ref), custom_call_target="tpu_custom_call" | custom-call | tf_op jit(solution)/shard_map/put_out/pallas_call | solution.py:403

commit v4 on v3

--- a/solution.py
+++ b/solution.py
@@ -116,7 +116,7 @@
     leaf_hbm, occ_hbm, angle_hbm, need3_hbm, need4_hbm,
     low_out, cone_out,
     leaf, occ, keep, angle, need3, need4, both, weight, part, got, mine, theirs, near, far, four,
-    in_sem, send, recv, send2, recv2, ready,
+    in_sem, send, recv, recv2, ready,
 ):
     groups = halves * blks
     half, blk, sub = lax.axis_index("half"), lax.axis_index("blk"), lax.axis_index("sub")
@@ -154,15 +154,46 @@
 
         each(0, blks, plane)
 
+    level = lax.rem(2 * blk + 1, blks)
+
+    def beside(wanted, act):
+        def device(t):
+            @pl.when(wanted(sub_of(t), sub))
+            def _():
+                act(level * subs + t)
+
+        each(0, subs, device)
+
     def greet(semaphore):
         return lambda d: pl.semaphore_signal(semaphore, inc=1, device_id=peer(d), device_id_type=MESH)
 
+    def across(t):
+        return {"blk": blk_of(0), "sub": sub_of(t)}
+
+    def greet_across(semaphore):
+        each(0, subs, lambda t: pl.semaphore_signal(semaphore, inc=1, device_id=across(t), device_id_type=MESH))
+
+    is_first, is_last = blk == 0, blk == blks - 1
+    is_end = lax.rem(blk, blks - 1) == 0
     barrier = pltpu.get_barrier_semaphore()
-    planes(operator.ge, greet(barrier))
+    planes(operator.gt, greet(barrier))
+    beside(operator.ge, greet(barrier))
+
+    @pl.when(is_first)
+    def _():
+        greet_across(barrier)
 
     table = axis_table()
     then = np.einsum("bij,qjk->bqik", table, table)
     build(table, then, (lax.rem(sub // 2, 2), lax.rem(sub, 2), (0, 1)), nodes, both)
+
+    pl.semaphore_wait(barrier, (blk + is_last.astype(jnp.int32)) * subs + sub + 1)
+    planes(operator.lt, lambda d: greet(ready.at[d // subs])(d))
+    beside(operator.lt, greet(ready.at[level]))
+
+    @pl.when(is_last)
+    def _():
+        greet_across(ready.at[0])
 
     pltpu.make_async_copy(occ_hbm, occ, in_sem.at[0]).wait()
     columns = jnp.transpose(occ[...].astype(F32))
@@ -176,21 +207,32 @@
         [both[2 * width * t : 2 * width * (t + 1), :] for t in range(family // 2)],
     )
 
-    pl.semaphore_wait(barrier, (blk + 1) * subs)
-
-    def copy(d):
-        there = peer(d)
+
+    def copy(d, there=None):
+        there = peer(d) if there is None else there
+        j = d // subs
         return pltpu.make_async_remote_copy(
             src_ref=part.at[pl.ds(pl.multiple_of(there["sub"] * per_sub, 8), per_sub)],
-            dst_ref=got.at[d // subs * subs + sub],
+            dst_ref=got.at[jnp.where(j == 0, half, j + 1) * subs + sub],
             send_sem=send.at[0],
-            recv_sem=recv.at[jnp.minimum(d // subs, 1)],
+            recv_sem=recv.at[jnp.minimum(j, 1)],
             device_id=there,
             device_id_type=MESH,
         )
 
-    planes(operator.le, lambda d: copy(d).start())
-    planes(operator.lt, lambda d: greet(ready.at[d // subs])(d))
+    def copy_across():
+        for to in range(halves):
+            each(0, subs, lambda t: copy(t, {"half": to, **across(t)}).start())
+
+    pl.when(is_last)(copy_across)
+    def inward(there):
+        @pl.when(jnp.logical_and(there < blk, there + blks - 1 != blk))
+        def _():
+            j = lax.rem(blk + there + 1, blks)
+            each(0, subs, lambda t: copy(j * subs + t).start())
+
+    each(0, blks - 1, inward)
+    beside(operator.le, lambda d: copy(d).start())
 
     build(table, then, (None, None, (None,)), nodes, weight)
 
@@ -242,14 +284,23 @@
     def outward(k):
         @pl.when(blk + k < blks)
         def _():
-            j = lax.rem(2 * blk + k + 1, blks)
-            pl.semaphore_wait(ready.at[j], subs)
-            each(0, subs, lambda t: copy(j * subs + t).start())
+            if k == blks - 1:
+                pl.semaphore_wait(ready.at[0], halves * subs)
+                copy_across()
+            else:
+                j = lax.rem(2 * blk + k + 1, blks)
+                pl.semaphore_wait(ready.at[j], subs)
+                each(0, subs, lambda t: copy(j * subs + t).start())
+
+    @pl.when(sub < subs - 1)
+    def _():
+        pl.semaphore_wait(ready.at[level], subs - 1 - sub)
+        beside(operator.gt, lambda d: copy(d).start())
 
     each(1, blks, outward)
 
-    def level_three(start, size):
-        boxes = [box for j in range(start, start + size) for box in (mine[j], theirs[j])]
+    def level_three(places):
+        boxes = [(mine, theirs)[own][j] for own, j in places]
         turned = [pltpu.roll(box, nodes, 1) for box in boxes]
         pieces = [
             jnp.concatenate(
@@ -261,7 +312,7 @@
             [jnp.concatenate(pieces[2 * t : 2 * t + 2], 1) for t in range(OCT // 2)],
             [weight[2 * width * t : 2 * width * (t + 1), :] for t in range(OCT // 2)],
         )
-        index = [first + blk_of(j) for j in range(start, start + size) for first in (other * blks, half * blks)]
+        index = [(other, half)[own] * blks + blk_of(j) for own, j in places]
         return [(g, result[i * padded : (i + 1) * padded]) for i, g in enumerate(index)]
 
     def rows_of(g, start, size):
@@ -269,16 +320,6 @@
         return weight[pl.ds(pl.multiple_of(base, nodes), size), :]
 
     def level_four(found):
-        turned = [far[0, g] * box + far[1, g] * pltpu.roll(box, nodes, 1) for g, box in found]
-        return product(
-            [jnp.concatenate(turned[i : i + 2], 1) for i in range(0, len(found), 2)],
-            [
-                jnp.concatenate([rows_of(g, 0, width) for g, _ in found[i : i + 2]], 0)
-                for i in range(0, len(found), 2)
-            ],
-        )
-
-    def level_four_last(found):
         return product(
             [jnp.concatenate([far[0, g] * box, far[1, g] * -box], 1) for g, box in found],
             [
@@ -289,51 +330,78 @@
 
     last, rest = pl.ds(0, 1), pl.ds(1, blks - 1)
 
-    def landed(k):
-        slots = got.at[pl.ds(0, subs)] if k == 0 else got.at[pl.ds(subs, (blks - 1) * subs)]
-        return pltpu.make_async_copy(slots, slots, recv.at[k])
-
-    def total(j):
-        mine[j] = functools.reduce(jnp.add, [got[j * subs + t] for t in range(subs)])
+    def landed(semaphore, first, count):
+        slots = got.at[pl.ds(first * subs, count * subs)]
+        pltpu.make_async_copy(slots, slots, semaphore).wait()
+
+    def total(slot):
+        return functools.reduce(jnp.add, [got[slot * subs + t] for t in range(subs)])
 
     def forward(k):
         boxes = last if k == 0 else rest
         return pltpu.make_async_remote_copy(
             src_ref=mine.at[boxes],
             dst_ref=theirs.at[boxes],
-            send_sem=send2.at[0],
-            recv_sem=recv2.at[k],
+            send_sem=send.at[0],
+            recv_sem=recv2.at[0],
             device_id={"half": other},
             device_id_type=MESH,
         )
 
-    landed(1).wait()
-    each(1, blks, total)
+    landed(recv.at[1], halves, blks - 1)
+    for j in range(1, blks):
+        mine[j] = total(j + 1)
     forward(1).start()
-    landed(0).wait()
-    total(0)
-    forward(0).start()
-    forward(1).wait_recv()
+
+    @pl.when(jnp.logical_not(is_end))
+    def _():
+        landed(recv.at[0], other, 1)
+        mine[0] = total(other)
+        forward(0).start()
+
     single = groups == OCT
+    direct = [(0, j) for j in range(1, blks)]
+    handed = [(1, j) for j in range(1, blks)] + [(0, 0), (1, 0)]
     if single:
-        early = level_four(level_three(1, blks - 1))
+        early = level_four(level_three(direct))
+
+    def handed_over(boxes):
+        pltpu.make_async_copy(theirs.at[boxes], theirs.at[boxes], recv2.at[0]).wait()
+
+    @pl.when(is_end)
+    def _():
+        handed_over(rest)
+        landed(recv.at[0], 0, halves)
+        mine[0] = total(other)
+        theirs[0] = total(half)
+
+    @pl.when(jnp.logical_not(is_end))
+    def _():
+        handed_over(pl.ds(0, blks))
+
+    if single:
+        cone_out[:, 0, :] = ((early + level_four(level_three(handed))) * keep4[0])[:cones]
     else:
         four[...] = jnp.zeros_like(four)
-        for start in range(1, blks, 3):
-            for g, box in level_three(start, min(3, blks - start)):
-                four[g // OCT] += level_four_last([(g, box)])
-    forward(0).wait_recv()
-    low_out[...] = theirs[lax.rem(2 * blk + 1, blks)]
-    if single:
-        cone_out[:, 0, :] = ((early + level_four_last(level_three(0, 1))) * keep4[0])[:cones]
-    else:
-        for g, box in level_three(0, 1):
-            four[g // OCT] += level_four_last([(g, box)])
+        together = direct + handed
+        for start in range(0, len(together), 6):
+            for g, box in level_three(together[start : start + 6]):
+                four[g // OCT] += level_four([(g, box)])
         for q in range(groups // OCT):
             cone_out[:, q, :] = (four[q] * keep4[q])[:cones]
-
-    pltpu.make_async_copy(got, got, send.at[0]).wait()
-    pltpu.make_async_copy(mine, mine, send2.at[0]).wait()
+    low_out[...] = theirs[level]
+
+    def sent(count):
+        slots = got.at[pl.ds(0, count)]
+        pltpu.make_async_copy(slots, slots, send.at[0]).wait()
+
+    @pl.when(is_end)
+    def _():
+        sent((blks + 1) * subs + blks - 1)
+
+    @pl.when(jnp.logical_not(is_end))
+    def _():
+        sent(blks * subs + blks)
 
 
 def put_out(low_ref, cone_ref, low_out, cone_out, sems):
@@ -383,7 +451,7 @@
                 pltpu.VMEM((family * width, 2 * width), BF16),
                 pltpu.VMEM((OCT * width, 2 * width), BF16),
                 pltpu.VMEM((pairs, width), F32),
-                pltpu.VMEM((blks * subs, per_sub, width), F32),
+                pltpu.VMEM(((blks + 1) * subs + blks, per_sub, width), F32),
                 pltpu.VMEM((blks, per_sub, width), F32),
                 pltpu.VMEM((blks, per_sub, width), F32),
                 pltpu.VMEM((2, OCT, padded, width), F32),
@@ -393,7 +461,6 @@
                 pltpu.SemaphoreType.DMA((1,)),
                 pltpu.SemaphoreType.DMA((2,)),
                 pltpu.SemaphoreType.DMA((1,)),
-                pltpu.SemaphoreType.DMA((2,)),
                 pltpu.SemaphoreType.REGULAR((blks,)),
             ],
             compiler_params=pltpu.CompilerParams(collective_id=0, has_side_effects=True),

time: 12.3 us -> 11.9 us (0.967)
  Pallas kernels: 11.5 us -> 11.1 us
    pallas_call x1, Pallas kernels: 10.9 us -> 10.5 us  [local(): pl.pallas_call(functools.partial(kernel, halves, blks, subs, cones), out_...]
where the time goes in v4:
time: 11.9 us; the launch traced here: 11.7 us
  Pallas kernels  11.1 us (93%)
  between operations  0.64 us (5%)
    pallas_call x1, Pallas kernels, local(): pl.pallas_call(functools.partial(kernel, halves, blks, subs, cones), out_...  10.5 us
    pallas_call x1, Pallas kernels, local(): pl.pallas_call(put_out, out_shape=[jax.ShapeDtypeStruct(value.shape, F32)...  0.61 us

profile of v4, /device:TPU:0, one launch (start us, length us, event | category | flops | bytes accessed | tf_op | source)
XLA Modules:
  0.0 11.7 jit_solution(16180620231146601788)
XLA Ops:
  0.6 10.5 %upward.1 = (f32[8,128]{1,0:T(8,128)S(1)}, f32[6,1,128]{2,1,0:T(1,128)S(1)}) custom-call(f32[32,16,128]{2,1,0:T(8,128)} %bitcast.3, s32[4,128]{1,0:T(4,128)} %bitcast.4, f32[2,48]{1,0:T(2,128)} %angle_hbm.1, s32[6,8]{1,0:T(8,128)} %need3_hbm.1, s32[1,6]{1,0:T(1,128)} %bitcast.5), custom_call_target="tpu_custom_call" | custom-call | tf_op jit(solution)/shard_map/upward/pallas_call | solution.py:436
  11.1 0.6 %put_out.1 = (f32[8,128]{1,0:T(8,128)}, f32[6,1,128]{2,1,0:T(1,128)}) custom-call(f32[8,128]{1,0:T(8,128)S(1)} %get-tuple-element.4.low_ref, f32[6,1,128]{2,1,0:T(1,128)S(1)} %get-tuple-element.5.cone_ref), custom_call_target="tpu_custom_call" | custom-call | tf_op jit(solution)/shard_map/put_out/pallas_call | solution.py:470

commit v5 on v4

--- a/solution.py
+++ b/solution.py
@@ -44,9 +44,8 @@
 
 
 def split_rows(value):
-    high = value.astype(BF16)
-    low = (value - high.astype(F32)).astype(BF16)
-    return jnp.concatenate([high, low], 0)
+    high = value.astype(BF16).astype(F32)
+    return jnp.concatenate([high, value - high], 0).astype(BF16)
 
 
 def fold(acc, rows, width):
@@ -101,18 +100,53 @@
             place[pl.ds((r * OCT + o) * 2 * nodes, 2 * nodes), :] = jnp.concatenate([high, low], 1)
 
 
-def product(tiles, weights):
+def push(weights, t, register):
+    pltpu.matmul_push_rhs(weights(t), staging_register=register, mxu_index=t % 2)
+
+
+def stage(sums, weights):
+    for t in range(2):
+        push(weights, t, 0)
+        pltpu.matmul_acc_lhs(sums[t], jnp.zeros(sums[t].shape, BF16), load_staged_rhs=0)
+    for t in range(2, 6):
+        push(weights, t, t // 2 - 1)
+
+
+def staged_product(sums, tiles, weights):
+    for t, tile in enumerate(tiles):
+        pltpu.matmul_acc_lhs(sums[t % 2], split_rows(tile), load_staged_rhs=(None, 0, 1, 0)[t // 2])
+        if t // 2 == 1:
+            push(weights, t + 4, 0)
+    return collect(sums, tiles)
+
+
+def product(sums, tiles, weights):
+    for t, tile in enumerate(tiles):
+        push(weights, t, t // 2 % 2)
+        pltpu.matmul_acc_lhs(sums[t % 2], split_rows(tile), load_staged_rhs=t // 2 % 2)
+    return collect(sums, tiles)
+
+
+def collect(sums, tiles):
     rows, width = tiles[0].shape
-    sums = [None, None]
-    for t, (tile, block) in enumerate(zip(tiles, weights)):
-        term = jnp.dot(split_rows(tile), block, preferred_element_type=F32)
-        sums[t % 2] = term if sums[t % 2] is None else sums[t % 2] + term
-    halves = [fold(value, rows, width // 2) for value in sums if value is not None]
-    return functools.reduce(jnp.add, halves)
-
-
-def kernel(
-    halves, blks, subs, cones,
+    parts = [fold(pltpu.matmul_pop(total), rows, width // 2) for total in sums[: len(tiles)]]
+    return functools.reduce(jnp.add, parts)
+
+
+def kernel(halves, blks, subs, cones, sizes, *refs):
+    specs = [pltpu.ACC(unit)((rows, 2 * refs[0].shape[-1]), F32) for rows in sizes for unit in range(2)]
+
+    def inside(*totals):
+        for total in totals:
+            pltpu.matmul_pop(total)
+        sums = {rows: totals[2 * i : 2 * i + 2] for i, rows in enumerate(sizes)}
+        upward(halves, blks, subs, cones, sums, *refs)
+
+    pl.run_scoped(inside, *specs)
+
+
+def upward(
+    halves, blks, subs, cones, sums,
     leaf_hbm, occ_hbm, angle_hbm, need3_hbm, need4_hbm,
     low_out, cone_out,
     leaf, occ, keep, angle, need3, need4, both, weight, part, got, mine, theirs, near, far, four,
@@ -188,25 +222,27 @@
     build(table, then, (lax.rem(sub // 2, 2), lax.rem(sub, 2), (0, 1)), nodes, both)
 
     pl.semaphore_wait(barrier, (blk + is_last.astype(jnp.int32)) * subs + sub + 1)
+
+    @pl.when(is_last)
+    def _():
+        greet_across(ready.at[0])
+
     planes(operator.lt, lambda d: greet(ready.at[d // subs])(d))
     beside(operator.lt, greet(ready.at[level]))
-
-    @pl.when(is_last)
-    def _():
-        greet_across(ready.at[0])
-
     pltpu.make_async_copy(occ_hbm, occ, in_sem.at[0]).wait()
     columns = jnp.transpose(occ[...].astype(F32))
     for i in range(pairs * family // 8):
         rows8 = columns[8 * (i % 16) : 8 * (i % 16) + 8, i // 16 : i // 16 + 1]
         keep[pl.ds(i % 2 * 8 * pairs + i // 2, 8, stride=pairs), :] = jnp.broadcast_to(rows8, (8, width))
+    def first_weights(t):
+        return both[2 * width * t : 2 * width * (t + 1), :]
+
+    stage(sums[2 * pairs], first_weights)
     pltpu.make_async_copy(leaf, leaf, in_sem.at[1]).wait()
     masked = [leaf[q * pairs : (q + 1) * pairs, :] * keep[q * pairs : (q + 1) * pairs, :] for q in range(family)]
-    part[...] = product(
-        [jnp.concatenate(masked[2 * t : 2 * t + 2], 1) for t in range(family // 2)],
-        [both[2 * width * t : 2 * width * (t + 1), :] for t in range(family // 2)],
+    part[...] = staged_product(
+        sums[2 * pairs], [jnp.concatenate(masked[2 * t : 2 * t + 2], 1) for t in range(family // 2)], first_weights
     )
-
 
     def copy(d, there=None):
         there = peer(d) if there is None else there
@@ -220,11 +256,14 @@
             device_id_type=MESH,
         )
 
-    def copy_across():
-        for to in range(halves):
+    def copy_across(order):
+        for to in order:
             each(0, subs, lambda t: copy(t, {"half": to, **across(t)}).start())
 
-    pl.when(is_last)(copy_across)
+    @pl.when(is_last)
+    def _():
+        copy_across(range(halves))
+
     def inward(there):
         @pl.when(jnp.logical_and(there < blk, there + blks - 1 != blk))
         def _():
@@ -286,7 +325,7 @@
         def _():
             if k == blks - 1:
                 pl.semaphore_wait(ready.at[0], halves * subs)
-                copy_across()
+                copy_across(reversed(range(halves)))
             else:
                 j = lax.rem(2 * blk + k + 1, blks)
                 pl.semaphore_wait(ready.at[j], subs)
@@ -299,34 +338,32 @@
 
     each(1, blks, outward)
 
-    def level_three(places):
+    def rows_of(base, start, size):
+        return weight[pl.ds(pl.multiple_of(base + start, nodes), size), :]
+
+    def turning(o):
+        base = lax.rem(o, OCT) * width
+        return jnp.concatenate([rows_of(base, 0, width), rows_of(base, nodes, nodes), rows_of(base, 0, nodes)], 0)
+
+    def level_three(places, multiply):
         boxes = [(mine, theirs)[own][j] for own, j in places]
-        turned = [pltpu.roll(box, nodes, 1) for box in boxes]
-        pieces = [
+        tiles = [
             jnp.concatenate(
-                [near[0, o] * box[o : o + 1, :] + near[1, o] * turn[o : o + 1, :] for box, turn in zip(boxes, turned)], 0
+                [
+                    jnp.concatenate([near[0, o] * box[o : o + 1, :], near[1, o] * -box[o : o + 1, :]], 1)
+                    for box in boxes
+                ],
+                0,
             )
             for o in range(OCT)
         ]
-        result = product(
-            [jnp.concatenate(pieces[2 * t : 2 * t + 2], 1) for t in range(OCT // 2)],
-            [weight[2 * width * t : 2 * width * (t + 1), :] for t in range(OCT // 2)],
-        )
+        result = multiply(sums[2 * padded * len(places)], tiles, turning)
         index = [(other, half)[own] * blks + blk_of(j) for own, j in places]
         return [(g, result[i * padded : (i + 1) * padded]) for i, g in enumerate(index)]
 
-    def rows_of(g, start, size):
-        base = lax.rem(g, OCT) * width + start
-        return weight[pl.ds(pl.multiple_of(base, nodes), size), :]
-
     def level_four(found):
-        return product(
-            [jnp.concatenate([far[0, g] * box, far[1, g] * -box], 1) for g, box in found],
-            [
-                jnp.concatenate([rows_of(g, 0, width), rows_of(g, nodes, nodes), rows_of(g, 0, nodes)], 0)
-                for g, _ in found
-            ],
-        )
+        tiles = [jnp.concatenate([far[0, g] * box, far[1, g] * -box], 1) for g, box in found]
+        return product(sums[2 * padded], tiles, lambda t: turning(found[t][0]))
 
     last, rest = pl.ds(0, 1), pl.ds(1, blks - 1)
 
@@ -363,7 +400,8 @@
     direct = [(0, j) for j in range(1, blks)]
     handed = [(1, j) for j in range(1, blks)] + [(0, 0), (1, 0)]
     if single:
-        early = level_four(level_three(direct))
+        early = level_four(level_three(direct, product))
+        stage(sums[2 * padded * len(handed)], turning)
 
     def handed_over(boxes):
         pltpu.make_async_copy(theirs.at[boxes], theirs.at[boxes], recv2.at[0]).wait()
@@ -380,12 +418,12 @@
         handed_over(pl.ds(0, blks))
 
     if single:
-        cone_out[:, 0, :] = ((early + level_four(level_three(handed))) * keep4[0])[:cones]
+        cone_out[:, 0, :] = ((early + level_four(level_three(handed, staged_product))) * keep4[0])[:cones]
     else:
         four[...] = jnp.zeros_like(four)
         together = direct + handed
         for start in range(0, len(together), 6):
-            for g, box in level_three(together[start : start + 6]):
+            for g, box in level_three(together[start : start + 6], product):
                 four[g // OCT] += level_four([(g, box)])
         for q in range(groups // OCT):
             cone_out[:, q, :] = (four[q] * keep4[q])[:cones]
@@ -428,13 +466,15 @@
         padded = -(-cones // 8) * 8
         assert per_sub == OCT and need3.shape[1] == groups and halves == 2 and subs * 2 == OCT
         assert width == 2 * ORDER**3 and blks % 2 == 0
+        boxes = (blks - 1, blks + 1) if groups == OCT else (6, 2 * blks % 6)
+        sizes = sorted({2 * pairs, 2 * padded} | {2 * padded * count for count in boxes if count})
         leaf = leaf.reshape(pairs, family, width)
         occupied = occupied.reshape(rows // 128, 128)
         need4 = need4.T
         vmem = pl.BlockSpec(memory_space=pltpu.VMEM)
         anywhere = pl.BlockSpec(memory_space=pl.ANY)
         results = pl.pallas_call(
-            functools.partial(kernel, halves, blks, subs, cones),
+            functools.partial(kernel, halves, blks, subs, cones, sizes),
             out_shape=(
                 pltpu.VMEM((per_sub, width), F32),
                 pltpu.VMEM((cones, groups // OCT, width), F32),

time: 11.9 us -> 11.8 us (level)
  no operation moved by 1% of the time
where the time goes in v5:
time: 11.8 us; the launch traced here: 11.6 us
  Pallas kernels  11 us (93%)
  between operations  0.64 us (5%)
    pallas_call x1, Pallas kernels, local(): pl.pallas_call(functools.partial(kernel, halves, blks, subs, cones, sizes...  10.4 us
    pallas_call x1, Pallas kernels, local(): pl.pallas_call(put_out, out_shape=[jax.ShapeDtypeStruct(value.shape, F32)...  0.61 us

profile of v5, /device:TPU:0, one launch (start us, length us, event | category | flops | bytes accessed | tf_op | source)
XLA Modules:
  0.0 11.6 jit_solution(16502706844702191663)
XLA Ops:
  0.6 10.4 %upward.1 = (f32[8,128]{1,0:T(8,128)S(1)}, f32[6,1,128]{2,1,0:T(1,128)S(1)}) custom-call(f32[32,16,128]{2,1,0:T(8,128)} %bitcast.3, s32[4,128]{1,0:T(4,128)} %bitcast.4, f32[2,48]{1,0:T(2,128)} %refs_2_.1, s32[6,8]{1,0:T(8,128)} %refs_3_.1, s32[1,6]{1,0:T(1,128)} %bitcast.5), custom_call_target="tpu_custom_call" | custom-call | tf_op jit(solution)/shard_map/upward/pallas_call | solution.py:476
  11.0 0.6 %put_out.1 = (f32[8,128]{1,0:T(8,128)}, f32[6,1,128]{2,1,0:T(1,128)}) custom-call(f32[8,128]{1,0:T(8,128)S(1)} %get-tuple-element.4.low_ref, f32[6,1,128]{2,1,0:T(1,128)S(1)} %get-tuple-element.5.cone_ref), custom_call_target="tpu_custom_call" | custom-call | tf_op jit(solution)/shard_map/put_out/pallas_call | solution.py:510

commit v6 on v5

--- a/solution.py
+++ b/solution.py
@@ -230,10 +230,17 @@
     planes(operator.lt, lambda d: greet(ready.at[d // subs])(d))
     beside(operator.lt, greet(ready.at[level]))
     pltpu.make_async_copy(occ_hbm, occ, in_sem.at[0]).wait()
-    columns = jnp.transpose(occ[...].astype(F32))
-    for i in range(pairs * family // 8):
-        rows8 = columns[8 * (i % 16) : 8 * (i % 16) + 8, i // 16 : i // 16 + 1]
-        keep[pl.ds(i % 2 * 8 * pairs + i // 2, 8, stride=pairs), :] = jnp.broadcast_to(rows8, (8, width))
+    lane = lax.broadcasted_iota(jnp.int32, (8, width), 1)
+    own = lane // family == lax.broadcasted_iota(jnp.int32, (8, width), 0)
+    flags = occ[...] << lax.rem(lane, family)[: occ.shape[0]]
+    taken = [
+        jnp.sum(jnp.where(own, jnp.broadcast_to(flags[i : i + 1].astype(F32), (8, width)), 0.0), 1, keepdims=True)
+        for i in range(pairs // 8)
+    ]
+    taken = jnp.broadcast_to(jnp.concatenate(taken, 0).astype(jnp.int32), (pairs, width))
+    for q in range(family):
+        keep[q * pairs : (q + 1) * pairs, :] = jnp.where((taken & (1 << q)) != 0, 1.0, 0.0)
+
     def first_weights(t):
         return both[2 * width * t : 2 * width * (t + 1), :]
 

time: 11.8 us -> 11.7 us (level)
  no operation moved by 1% of the time
where the time goes in v6:
time: 11.7 us; the launch traced here: 11.5 us
  Pallas kernels  10.9 us (93%)
  between operations  0.64 us (5%)
    pallas_call x1, Pallas kernels, local(): pl.pallas_call(functools.partial(kernel, halves, blks, subs, cones, sizes...  10.3 us
    pallas_call x1, Pallas kernels, local(): pl.pallas_call(put_out, out_shape=[jax.ShapeDtypeStruct(value.shape, F32)...  0.61 us

profile of v6, /device:TPU:0, one launch (start us, length us, event | category | flops | bytes accessed | tf_op | source)
XLA Modules:
  0.0 11.5 jit_solution(3968535081212580407)
XLA Ops:
  0.6 10.3 %upward.1 = (f32[8,128]{1,0:T(8,128)S(1)}, f32[6,1,128]{2,1,0:T(1,128)S(1)}) custom-call(f32[32,16,128]{2,1,0:T(8,128)} %bitcast.3, s32[4,128]{1,0:T(4,128)} %bitcast.4, f32[2,48]{1,0:T(2,128)} %refs_2_.1, s32[6,8]{1,0:T(8,128)} %refs_3_.1, s32[1,6]{1,0:T(1,128)} %bitcast.5), custom_call_target="tpu_custom_call" | custom-call | tf_op jit(solution)/shard_map/upward/pallas_call | solution.py:483
  10.9 0.6 %put_out.1 = (f32[8,128]{1,0:T(8,128)}, f32[6,1,128]{2,1,0:T(1,128)}) custom-call(f32[8,128]{1,0:T(8,128)S(1)} %get-tuple-element.4.low_ref, f32[6,1,128]{2,1,0:T(1,128)S(1)} %get-tuple-element.5.cone_ref), custom_call_target="tpu_custom_call" | custom-call | tf_op jit(solution)/shard_map/put_out/pallas_call | solution.py:517

commit v7 on v6

--- a/solution.py
+++ b/solution.py
@@ -150,7 +150,7 @@
     leaf_hbm, occ_hbm, angle_hbm, need3_hbm, need4_hbm,
     low_out, cone_out,
     leaf, occ, keep, angle, need3, need4, both, weight, part, got, mine, theirs, near, far, four,
-    in_sem, send, recv, recv2, ready,
+    in_sem, recv, recv2, ready,
 ):
     groups = halves * blks
     half, blk, sub = lax.axis_index("half"), lax.axis_index("blk"), lax.axis_index("sub")
@@ -163,11 +163,9 @@
     for q in range(family):
         pltpu.make_async_copy(leaf_hbm.at[:, q], leaf.at[pl.ds(q * pairs, pairs)], in_sem.at[1]).start()
     loads = [
-        pltpu.make_async_copy(src, dst, in_sem.at[2 + i])
-        for i, (src, dst) in enumerate([(angle_hbm, angle), (need3_hbm, need3), (need4_hbm, need4)])
+        pltpu.make_async_copy(src, dst, in_sem.at[0])
+        for src, dst in [(angle_hbm, angle), (need3_hbm, need3), (need4_hbm, need4)]
     ]
-    for load in loads:
-        load.start()
 
     other = halves - 1 - half
 
@@ -230,6 +228,7 @@
     planes(operator.lt, lambda d: greet(ready.at[d // subs])(d))
     beside(operator.lt, greet(ready.at[level]))
     pltpu.make_async_copy(occ_hbm, occ, in_sem.at[0]).wait()
+    loads[0].start()
     lane = lax.broadcasted_iota(jnp.int32, (8, width), 1)
     own = lane // family == lax.broadcasted_iota(jnp.int32, (8, width), 0)
     flags = occ[...] << lax.rem(lane, family)[: occ.shape[0]]
@@ -257,19 +256,19 @@
         return pltpu.make_async_remote_copy(
             src_ref=part.at[pl.ds(pl.multiple_of(there["sub"] * per_sub, 8), per_sub)],
             dst_ref=got.at[jnp.where(j == 0, half, j + 1) * subs + sub],
-            send_sem=send.at[0],
+            send_sem=in_sem.at[1],
             recv_sem=recv.at[jnp.minimum(j, 1)],
             device_id=there,
             device_id_type=MESH,
         )
 
-    def copy_across(order):
-        for to in order:
-            each(0, subs, lambda t: copy(t, {"half": to, **across(t)}).start())
+    def copy_across(to, t):
+        copy(t, {"half": to, **across(t)}).start()
 
     @pl.when(is_last)
     def _():
-        copy_across(range(halves))
+        for to in range(halves):
+            each(0, subs, lambda t: copy_across(to, t))
 
     def inward(there):
         @pl.when(jnp.logical_and(there < blk, there + blks - 1 != blk))
@@ -280,9 +279,9 @@
     each(0, blks - 1, inward)
     beside(operator.le, lambda d: copy(d).start())
 
+    loads[0].wait()
+    loads[1].start()
     build(table, then, (None, None, (None,)), nodes, weight)
-
-    loads[0].wait()
     padded = near.shape[2]
     count = angle.shape[1]
     pick = lax.broadcasted_iota(jnp.int32, (padded, count), 1) == (
@@ -296,8 +295,8 @@
     points = [float(value) for value in chebyshev_points(ORDER)]
     places = [choose(digit_of(lane, ORDER**power), points) for power in (2, 1, 0)]
     sign = jnp.where(lane < nodes, -1.0, 1.0)
-    for load in loads[1:]:
-        load.wait()
+    loads[1].wait()
+    loads[2].start()
 
     def widen(value):
         fill = padded - cones
@@ -318,21 +317,12 @@
             kept = keep3[:, g : g + 1]
             far[0, g] = (1.0 - 2.0 * sine * sine) * kept
             far[1, g] = 2.0 * sine * cosine * sign * kept
-    lanes4 = need4.shape[1]
-    diagonal = lax.broadcasted_iota(jnp.int32, (padded, lanes4), 0) == lax.broadcasted_iota(
-        jnp.int32, (padded, lanes4), 1
-    )
-    keep4 = [
-        jnp.sum(jnp.where(diagonal, need4[q : q + 1, :].astype(F32), 0.0), 1, keepdims=True)
-        for q in range(groups // OCT)
-    ]
-
     def outward(k):
         @pl.when(blk + k < blks)
         def _():
             if k == blks - 1:
                 pl.semaphore_wait(ready.at[0], halves * subs)
-                copy_across(reversed(range(halves)))
+                each(0, subs, lambda t: [copy_across(to, t) for to in reversed(range(halves))])
             else:
                 j = lax.rem(2 * blk + k + 1, blks)
                 pl.semaphore_wait(ready.at[j], subs)
@@ -386,7 +376,7 @@
         return pltpu.make_async_remote_copy(
             src_ref=mine.at[boxes],
             dst_ref=theirs.at[boxes],
-            send_sem=send.at[0],
+            send_sem=in_sem.at[1],
             recv_sem=recv2.at[0],
             device_id={"half": other},
             device_id_type=MESH,
@@ -402,6 +392,16 @@
         landed(recv.at[0], other, 1)
         mine[0] = total(other)
         forward(0).start()
+
+    loads[2].wait()
+    lanes4 = need4.shape[1]
+    diagonal = lax.broadcasted_iota(jnp.int32, (padded, lanes4), 0) == lax.broadcasted_iota(
+        jnp.int32, (padded, lanes4), 1
+    )
+    keep4 = [
+        jnp.sum(jnp.where(diagonal, need4[q : q + 1, :].astype(F32), 0.0), 1, keepdims=True)
+        for q in range(groups // OCT)
+    ]
 
     single = groups == OCT
     direct = [(0, j) for j in range(1, blks)]
@@ -438,7 +438,7 @@
 
     def sent(count):
         slots = got.at[pl.ds(0, count)]
-        pltpu.make_async_copy(slots, slots, send.at[0]).wait()
+        pltpu.make_async_copy(slots, slots, in_sem.at[1]).wait()
 
     @pl.when(is_end)
     def _():
@@ -504,8 +504,7 @@
                 pltpu.VMEM((2, OCT, padded, width), F32),
                 pltpu.VMEM((2, groups, padded, width), F32),
                 pltpu.VMEM((groups // OCT, padded, width), F32),
-                pltpu.SemaphoreType.DMA((5,)),
-                pltpu.SemaphoreType.DMA((1,)),
+                pltpu.SemaphoreType.DMA((2,)),
                 pltpu.SemaphoreType.DMA((2,)),
                 pltpu.SemaphoreType.DMA((1,)),
                 pltpu.SemaphoreType.REGULAR((blks,)),

time: 11.7 us -> 11.7 us (level)
  no operation moved by 1% of the time
where the time goes in v7:
time: 11.7 us; the launch traced here: 11.5 us
  Pallas kernels  10.8 us (92%)
  between operations  0.64 us (5%)
    pallas_call x1, Pallas kernels, local(): pl.pallas_call(functools.partial(kernel, halves, blks, subs, cones, sizes...  10.2 us
    pallas_call x1, Pallas kernels, local(): pl.pallas_call(put_out, out_shape=[jax.ShapeDtypeStruct(value.shape, F32)...  0.61 us

profile of v7, /device:TPU:0, one launch (start us, length us, event | category | flops | bytes accessed | tf_op | source)
XLA Modules:
  0.0 11.5 jit_solution(5111180138838245197)
XLA Ops:
  0.6 10.2 %upward.1 = (f32[8,128]{1,0:T(8,128)S(1)}, f32[6,1,128]{2,1,0:T(1,128)S(1)}) custom-call(f32[32,16,128]{2,1,0:T(8,128)} %bitcast.3, s32[4,128]{1,0:T(4,128)} %bitcast.4, f32[2,48]{1,0:T(2,128)} %refs_2_.1, s32[6,8]{1,0:T(8,128)} %refs_3_.1, s32[1,6]{1,0:T(1,128)} %bitcast.5), custom_call_target="tpu_custom_call" | custom-call | tf_op jit(solution)/shard_map/upward/pallas_call | solution.py:483
  10.9 0.6 %put_out.1 = (f32[8,128]{1,0:T(8,128)}, f32[6,1,128]{2,1,0:T(1,128)}) custom-call(f32[8,128]{1,0:T(8,128)S(1)} %get-tuple-element.4.low_ref, f32[6,1,128]{2,1,0:T(1,128)S(1)} %get-tuple-element.5.cone_ref), custom_call_target="tpu_custom_call" | custom-call | tf_op jit(solution)/shard_map/put_out/pallas_call | solution.py:516
